TPU v7x, 32 devices: a whole 2x2x4 slice. The times are simulated.
32 devices in a mesh: tm: 16 (over z, y, core), space: 2 (over x).
Axes of the slice: x: 2, y: 2, z: 4, core: 2. Of those that a mesh axis runs over, the one named last changes fastest.
Arguments:
- forcing: float32 [32, 128, 128, 128], P('tm', 'space'), may hold values from -24 to 24
- exponents: int32 [32], P('tm'), may hold values from 0 to 8
- mixing: float32 [32, 32], replicated, may hold values from -1 to 3, as said below
- unmixing: float32 [32, 32], replicated, may hold values from -1 to 1
Outputs:
- solution: float32 [32, 128, 128, 128], P('tm', 'space')
Inputs may be any that keep to these rules, and one draw needn't show every extreme that they name: unmixing is the inverse of mixing up to float32 rounding.
All inputs are finite; a program needn't handle non-finite values.
Results may differ from a plain program's by a relative error of at most 0.00027.
Values sent between devices are 32-bit elements; how exact they have to be, the bound alone decides.
A program may use at most 128 MiB of HBM per device.

v0:
```python
import jax
import jax.numpy as jnp
from jax import lax
from jax.sharding import PartitionSpec as P

exact_mode = lax.Precision.HIGHEST


def sine_matrix(length):
    ordinal = jnp.arange(length, dtype=jnp.float32) + 1.0
    angle_step = jnp.pi / (length + 1)
    return jnp.sqrt(2.0 / (length + 1.0)) * jnp.sin(
        angle_step * ordinal[:, None] * ordinal[None, :]
    )


def eigen_values(length):
    ordinal = jnp.arange(length, dtype=jnp.float32) + 1.0
    return 2.0 - 2.0 * jnp.cos(jnp.pi * ordinal / (length + 1))


def final_axis_product(values, matrix):
    return jnp.dot(values, matrix, precision=exact_mode)


def along_second(values, matrix):
    return jnp.einsum("tabc,ak->tkbc", values, matrix, precision=exact_mode)


def third_axis_product(values, matrix):
    return jnp.einsum("tabc,bk->takc", values, matrix, precision=exact_mode)


def body(forcing, exponents, mixing, unmixing):
    step_count = mixing.shape[0]
    length = forcing.shape[2]
    transform_matrix = sine_matrix(length)
    eigen_all = eigen_values(length)
    source = third_axis_product(final_axis_product(forcing, transform_matrix), transform_matrix)
    time_full = lax.all_to_all(source, "tm", split_axis=2, concat_axis=0, tiled=True)
    time_mixed_field = jnp.dot(
        unmixing, time_full.reshape(step_count, -1), precision=exact_mode
    ).reshape(time_full.shape)
    all_exponents = lax.all_gather(exponents, "tm", axis=0, tiled=True)
    all_shifts = 2.0 ** (all_exponents.astype(jnp.float32) / 4.0)
    columns = lax.all_to_all(time_mixed_field, "space", split_axis=3, concat_axis=1, tiled=True)
    middle_part = columns.shape[2]
    last_part = columns.shape[3]
    middle_start = lax.axis_index("tm") * middle_part
    last_start = lax.axis_index("space") * last_part
    eigen_middle = lax.dynamic_slice_in_dim(eigen_all, middle_start, middle_part)
    eigen_tail = lax.dynamic_slice_in_dim(eigen_all, last_start, last_part)
    spectral_field = along_second(columns, transform_matrix)
    denom = (
        all_shifts[:, None, None, None]
        + eigen_all[None, :, None, None]
        + eigen_middle[None, None, :, None]
        + eigen_tail[None, None, None, :]
    )
    spectral_field = along_second(spectral_field / denom, transform_matrix)
    time_back = lax.all_to_all(spectral_field, "space", split_axis=1, concat_axis=3, tiled=True)
    result = jnp.dot(mixing, time_back.reshape(step_count, -1), precision=exact_mode).reshape(
        time_back.shape
    )
    final = lax.all_to_all(result, "tm", split_axis=0, concat_axis=2, tiled=True)
    final = third_axis_product(final_axis_product(final, transform_matrix), transform_matrix)
    return final


def solution(mesh):
    placed = (P("tm", "space", None, None), P("tm"), P(), P())
    return jax.shard_map(
        body, mesh=mesh, in_specs=placed, out_specs=P("tm", "space", None, None), check_vma=False
    )
```

profile of v0, /device:TPU:0, one launch (start us, length us, event | category | flops | bytes accessed | tf_op | source)
XLA Modules:
  0.0 966.3 jit_solution(384593514422324114)
XLA Ops:
  0.0 11.6 %fusion.11 = f32[128,2,64,128]{3,0,2,1:T(8,128)S(1)} fusion(f32[2,64,128,128]{3,2,1,0:T(8,128)} %param.4, f32[128]{0:T(128)S(1)} %get-tuple-element.5, f32[128]{0:T(128)S(1)} %get-tuple-element.6), kind=kOutput, calls=%fused_computation.16 | convolution fusion | flops 3221258240 | bytes 16778240 | tf_op jit(solution)/shard_map/dot_general | solution.py:23
  25.5 189.2 %all_to_all.66 = f32[2,64,128,128]{3,1,0,2:T(8,128)S(1)} all-to-all(f32[2,64,128,128]{3,1,0,2:T(8,128)S(1)} %copy.30), channel_id=1, replica_groups=mesh['tm'=16,'space'=2] {'tm'}, dimensions={2} | all-to-all | bytes 16777216 | tf_op jit(solution)/shard_map/all_to_all | solution.py:40
  214.7 11.1 %copy.60 = f32[2,64,16,8,128]{4,3,1,0,2:T(8,128)} copy(f32[2,64,16,8,128]{4,1,0,3,2:T(8,128)S(1)} %bitcast.91) | data formatting | bytes 16777216 | tf_op jit(solution)/shard_map/all_to_all | solution.py:40
  233.2 10.4 %convolution_bitcast_fusion.2 = f32[4,8,512,128]{3,1,2,0:T(8,128)S(1)} fusion(f32[32,65536]{1,0:T(8,128)} %reshape.73, f32[32,32]{1,0:T(8,128)S(1)} %copy-done), kind=kOutput, calls=%fused_computation.12 | convolution fusion | flops 805306368 | bytes 16781312 | tf_op jit(solution)/shard_map/dot_general | solution.py:41
  248.6 16.7 %copy.32 = f32[32,64,8,128]{1,2,0,3:T(8,128)} copy(f32[32,64,8,128]{3,2,1,0:T(8,128)} %bitcast.90) | data formatting | bytes 16777216 | tf_op jit(solution)/shard_map/reshape | solution.py:43
  265.2 21.1 %reshape.88 = f32[2,1,1048576]{2,1,0:T(1,128)} reshape(f32[128,32,8,64]{3,2,1,0:T(8,128)} %bitcast.80) | data formatting | bytes 16777216
  295.2 12.1 %all-reduce = s32[32]{0:T(128)S(1)} all-reduce(s32[32]{0:T(128)S(1)} %dynamic-update-slice), channel_id=1, replica_groups=mesh['tm'=16,'space'=2] {'tm'}, use_global_device_ids=true, to_apply=%add | all-reduce | flops 32 | bytes 256
  307.5 79.7 %all-to-all-done.1 = f32[2,1,1048576]{2,1,0:T(1,128)} async-done(((f32[2,1,1048576]{2,1,0:T(1,128)}), f32[2,1,1048576]{2,1,0:T(1,128)}, u32[]{:S(2)}, u32[]{:S(2)}) %all-to-all-start.1) | async-done | bytes 8388640 | tf_op jit(solution)/shard_map/all_to_all | solution.py:46
  387.8 30.9 %reduce = f32[2,1048576]{1,0:T(2,128)} reduce(f32[2,1,1048576]{2,1,0:T(1,128)} %all-to-all-done.1, f32[]{:T(128)} %broadcast.86), dimensions={1}, to_apply=%all_to_all.51.reduce_sub_computation | reduce | bytes 16777220 | tf_op jit(solution)/shard_map/all_to_all | solution.py:46
  418.7 21.2 %reshape.89 = f32[128,32,8,64]{3,2,1,0:T(8,128)} reshape(f32[2,1048576]{1,0:T(2,128)} %reduce) | data formatting | bytes 16777216
  439.9 29.0 %copy.58 = f32[32,64,8,2,64]{1,3,4,2,0:T(2,128)} copy(f32[32,64,8,2,64]{1,2,0,4,3:T(8,128)} %bitcast.82) | data formatting | bytes 16777216 | tf_op jit(solution)/shard_map/all_to_all | solution.py:46
  468.9 16.3 %all_to_all.54 = f32[32,128,8,64]{1,3,2,0:T(8,128)} reshape(f32[32,2,64,8,64]{2,1,4,3,0:T(2,128)} %bitcast.83) | data formatting | bytes 16777216 | tf_op jit(solution)/shard_map/all_to_all | solution.py:46
  485.3 10.7 %fusion.13 = f32[128,16384]{0,1:S(1)} fusion(f32[128,16384]{0,1:T(8,128)} %bitcast.86, f32[128]{0:T(128)S(1)} %get-tuple-element.5, f32[128]{0:T(128)S(1)} %get-tuple-element.6), kind=kOutput, calls=%fused_computation.20 | convolution fusion | flops 3221258240 | bytes 16778240
  498.2 9.6 fusion.14
  507.8 16.2 %copy.37 = f32[32,128,8,64]{3,2,0,1:T(8,128)} copy(f32[32,128,8,64]{1,3,2,0:T(8,128)} %bitcast.87) | data formatting | bytes 16777216 | tf_op jit(solution)/shard_map/tabc,ak->tkbc/transpose | solution.py:27
  524.0 21.1 %reshape.90 = f32[2,1,1048576]{2,1,0:T(1,128)} reshape(f32[128,32,8,64]{3,2,1,0:T(8,128)} %bitcast.81) | data formatting | bytes 16777216
  545.1 103.9 %all_to_all.67 = f32[2,1,1048576]{2,1,0:T(1,128)} all-to-all(f32[2,1,1048576]{2,1,0:T(1,128)} %reshape.90), channel_id=1, replica_groups=mesh['tm'=16,'space'=2] {'space'}, dimensions={0} | all-to-all | bytes 16777216 | tf_op jit(solution)/shard_map/all_to_all | solution.py:61
  649.0 31.3 %reduce.1 = f32[2,1048576]{1,0:T(2,128)} reduce(f32[2,1,1048576]{2,1,0:T(1,128)} %all_to_all.67, f32[]{:T(128)} %broadcast.86), dimensions={1}, to_apply=%all_to_all.55.reduce_sub_computation | reduce | bytes 16777220 | tf_op jit(solution)/shard_map/all_to_all | solution.py:61
  680.4 21.2 %reshape.91 = f32[128,32,8,64]{3,2,1,0:T(8,128)} reshape(f32[2,1048576]{1,0:T(2,128)} %reduce.1) | data formatting | bytes 16777216
  701.6 28.8 %copy.59 = f32[32,2,64,8,64]{4,1,3,2,0:T(2,128)} copy(f32[32,2,64,8,64]{4,3,0,2,1:T(8,128)} %bitcast.84) | data formatting | bytes 16777216 | tf_op jit(solution)/shard_map/all_to_all | solution.py:61
  730.4 19.5 %reshape.75 = f32[32,65536]{1,0:T(8,128)} reshape(f32[32,64,8,2,64]{4,3,2,1,0:T(2,128)} %bitcast.85) | data formatting | bytes 16777216 | tf_op jit(solution)/shard_map/reshape | solution.py:62
  749.8 10.1 %convolution_bitcast_fusion.1 = f32[4,8,512,128]{3,1,2,0:T(8,128)S(1)} fusion(f32[32,65536]{1,0:T(8,128)} %reshape.75, f32[32,32]{1,0:T(8,128)S(1)} %copy-done.2), kind=kOutput, calls=%fused_computation.11 | convolution fusion | flops 805306368 | bytes 16781312 | tf_op jit(solution)/shard_map/dot_general | solution.py:62
  761.4 186.6 %all_to_all.68 = f32[32,64,8,128]{3,2,1,0:T(8,128)S(1)} all-to-all(f32[32,64,8,128]{3,2,1,0:T(8,128)S(1)} %bitcast.93), channel_id=1, replica_groups=mesh['tm'=16,'space'=2] {'tm'}, dimensions={0} | all-to-all | bytes 16777216 | tf_op jit(solution)/shard_map/all_to_all | solution.py:65
  956.0 10.1 %convolution_bitcast_fusion = f32[2,64,128,128]{3,2,1,0:T(8,128)} fusion(f32[2,64,128,128]{3,2,1,0:T(8,128)S(1)} %fusion, f32[128]{0:T(128)S(1)} %get-tuple-element.5, f32[128]{0:T(128)S(1)} %get-tuple-element.6), kind=kOutput, calls=%fused_computation.10 | convolution fusion | flops 3221258240 | bytes 16778240 | tf_op jit(solution)/shard_map/tabc,bk->takc/dot_general | solution.py:31
  (29 shorter events, 47.0 us)
Async XLA Ops:
  0.0 233.2 %copy-start = (f32[32,32]{1,0:T(8,128)S(1)}, f32[32,32]{1,0:T(8,128)}, u32[]{:S(2)}) copy-start(f32[32,32]{1,0:T(8,128)} %param.7) | copy-start | bytes 12292
  286.4 7.3 copy-start.4
  286.4 8.4 copy-start.3
  286.4 100.8 %all-to-all-start.1 = ((f32[2,1,1048576]{2,1,0:T(1,128)}), f32[2,1,1048576]{2,1,0:T(1,128)}, u32[]{:S(2)}, u32[]{:S(2)}) async-start(f32[2,1,1048576]{2,1,0:T(1,128)} %reshape.88), calls=%async_computation.1 | async-start | bytes 16777216 | tf_op jit(solution)/shard_map/all_to_all | solution.py:46
  730.4 19.5 %copy-start.2 = (f32[32,32]{1,0:T(8,128)S(1)}, f32[32,32]{1,0:T(8,128)}, u32[]{:S(2)}) copy-start(f32[32,32]{1,0:T(8,128)} %param.6) | copy-start | bytes 12292
  948.0 18.1 %copy-start.1 = (f32[32,32]{1,0:T(8,128)S(1)}, f32[32,32]{1,0:T(8,128)}, u32[]{:S(2)}) copy-start(f32[32,32]{1,0:T(8,128)} %param.7) | copy-start | bytes 12292
where the time goes:
time: 972 us; the launch traced here: 966 us
  blocking collectives  492 us (51%)
  local copies, waits for them, and re-layouts  243 us (25%)
  waiting for transfers between devices  79.7 us (8%)
  matrix products  79.3 us (8%)
  other arithmetic  64.7 us (7%)
    all_to_all x1, blocking collectives, body(): lax.all_to_all(source, 'tm', split_axis=2, concat_axis=0, tiled=True)  189 us
    all_to_all x1, blocking collectives, body(): lax.all_to_all(result, 'tm', split_axis=0, concat_axis=2, tiled=True)  187 us
    all_to_all x1, blocking collectives, body(): lax.all_to_all(spectral_field, 'space', split_axis=1, concat_axis=3, tile...  104 us
    unnamed x19, local copies, waits for them, and re-layouts  92.1 us
    all_to_all x1, waiting for transfers between devices, body(): lax.all_to_all(time_mixed_field, 'space', split_axis=3, concat_axis=1, ti...  79.7 us
    all_to_all x3, local copies, waits for them, and re-layouts, body(): lax.all_to_all(time_mixed_field, 'space', split_axis=3, concat_axis=1, ti...  45.9 us
    all_to_all x1, other arithmetic, body(): lax.all_to_all(spectral_field, 'space', split_axis=1, concat_axis=3, tile...  31.3 us
    all_to_all x1, other arithmetic, body(): lax.all_to_all(time_mixed_field, 'space', split_axis=3, concat_axis=1, ti...  30.9 us
  transfers between devices with their start and end apart: 1, of which 1 were waited for; matrix products, arithmetic and copies ran while one was open for 0% of the time, Pallas kernels for 0%

commit v1 on v0

v1 whole, which is shorter than its diff:
```python
import jax
import jax.numpy as jnp
from jax import lax
from jax.sharding import PartitionSpec as P

split_mode = lax.Precision.HIGH


def sine_matrix(length):
    ordinal = jnp.arange(length, dtype=jnp.float32) + 1.0
    angle_step = jnp.pi / (length + 1)
    return jnp.sqrt(2.0 / (length + 1.0)) * jnp.sin(
        angle_step * ordinal[:, None] * ordinal[None, :]
    )


def eigen_values(length):
    ordinal = jnp.arange(length, dtype=jnp.float32) + 1.0
    return 2.0 - 2.0 * jnp.cos(jnp.pi * ordinal / (length + 1))


def product(formula, left, right):
    return jnp.einsum(formula, left, right, precision=split_mode)


def body(times, slabs, forcing, exponents, mixing, unmixing):
    own_steps, slab, length, _ = forcing.shape
    devices = times * slabs
    rows = max(1, length // devices)
    pieces = max(1, devices // length)
    width = length // pieces
    everyone = ("tm", "space")
    sine = sine_matrix(length)
    eigen = eigen_values(length)
    all_exponents = lax.all_gather(exponents, "tm", axis=0, tiled=True)
    shifts = 2.0 ** (all_exponents.astype(jnp.float32) / 4.0)

    field = product("labc,ck->labk", forcing, sine)
    field = product("labk,bj->jlak", field, sine)
    field = field.reshape(length, own_steps, slab, pieces, width).transpose(0, 3, 1, 2, 4)
    field = field.reshape(length * pieces, own_steps, slab, width)
    field = lax.all_to_all(field, everyone, split_axis=0, concat_axis=0, tiled=True)
    field = field.reshape(times, slabs, rows, own_steps, slab, width)
    field = field.transpose(2, 0, 3, 1, 4, 5).reshape(rows, times * own_steps, length, width)

    field = product("lm,jmak->jlak", unmixing, field)
    field = product("jlak,ai->jlik", field, sine)
    device = lax.axis_index("tm") * slabs + lax.axis_index("space")
    own_rows = lax.dynamic_slice_in_dim(eigen, device * rows // pieces, rows)
    own_columns = lax.dynamic_slice_in_dim(eigen, device % pieces * width, width)
    denom = (
        shifts[None, :, None, None]
        + eigen[None, None, :, None]
        + own_rows[:, None, None, None]
        + own_columns[None, None, None, :]
    )
    field = product("jlik,ia->jlak", field / denom, sine)
    field = product("lm,jmak->jlak", mixing, field)

    field = field.reshape(rows, times, own_steps, slabs, slab, width)
    field = field.transpose(1, 3, 0, 2, 4, 5).reshape(length * pieces, own_steps, slab, width)
    field = lax.all_to_all(field, everyone, split_axis=0, concat_axis=0, tiled=True)
    field = field.reshape(length, pieces, own_steps, slab, width).transpose(0, 2, 3, 1, 4)
    field = field.reshape(length, own_steps, slab, length)
    field = product("jlak,jb->labk", field, sine)
    return product("labk,kc->labc", field, sine)


def solution(mesh):
    placed = (P("tm", "space", None, None), P("tm"), P(), P())

    def run(*arrays):
        return body(mesh.shape["tm"], mesh.shape["space"], *arrays)

    return jax.shard_map(
        run, mesh=mesh, in_specs=placed, out_specs=P("tm", "space", None, None), check_vma=False
    )
```

time: 972 us -> 468 us (0.48)
  local copies, waits for them, and re-layouts: 243 us -> 18.3 us
  blocking collectives: 492 us -> 373 us
  waiting for transfers between devices: 79.7 us -> 0.01 us
  other arithmetic: 64.7 us -> 0.21 us
  matrix products: 79.3 us -> 58.3 us
    all_to_all x3 -> x1, blocking collectives: 480 us -> 190 us  [body(): lax.all_to_all(field, everyone, split_axis=0, concat_axis=0, tiled=True)]
    unnamed x1, blocking collectives: 12.1 us -> 183 us
    unnamed x19 -> x13, local copies, waits for them, and re-layouts: 92.1 us -> 0.91 us
    all_to_all x5 -> x0, local copies, waits for them, and re-layouts: 85.8 us -> none  [the longest x3 45.9 us: body(): lax.all_to_all(time_mixed_field, 'space', split_axis=3, concat_axis=1, ti...]
    all_to_all x1, waiting for transfers between devices: 79.7 us -> 0.01 us  [body(): lax.all_to_all(field, everyone, split_axis=0, concat_axis=0, tiled=True)]
    all_to_all x2 -> x0, other arithmetic: 62.3 us -> none  [the longest x1 31.3 us: body(): lax.all_to_all(spectral_field, 'space', split_axis=1, concat_axis=3, tile...]
    reshape x3 -> x1, local copies, waits for them, and re-layouts: 43.6 us -> 4.86 us  [body(): field = field.reshape(rows, times, own_steps, slabs, slab, width)]
    unnamed x2 -> x0, matrix products: 20.3 us -> none
  transfers between devices with their start and end apart: 1 -> 1, of which waited for: 1 -> 0; matrix products, arithmetic and copies ran while one was open for 0% -> 0% of each run, Pallas kernels for 0% -> 0%
where the time goes in v1:
time: 468 us; the launch traced here: 459 us
  blocking collectives  373 us (80%)
  matrix products  58.3 us (12%)
  local copies, waits for them, and re-layouts  18.3 us (4%)
  starting transfers between devices  7.46 us (2%)
    all_to_all x1, blocking collectives, body(): lax.all_to_all(field, everyone, split_axis=0, concat_axis=0, tiled=True)  190 us
    unnamed x1, blocking collectives  183 us
    dot_general x8, matrix products, product(): return jnp.einsum(formula, left, right, precision=split_mode)  58.3 us
  transfers between devices with their start and end apart: 1, of which 0 were waited for; matrix products, arithmetic and copies ran while one was open for 0% of the time, Pallas kernels for 0%

profile of v1, /device:TPU:0, one launch (start us, length us, event | category | flops | bytes accessed | tf_op | source)
XLA Modules:
  0.0 458.7 jit_solution(13602219270178209574)
XLA Ops:
  0.0 0.0 copy-start
  0.0 6.9 %fusion.21 = f32[128,2,64,128]{3,0,2,1:T(8,128)S(1)} fusion(f32[2,64,128,128]{3,2,1,0:T(8,128)} %param.4, f32[128]{0:T(128)S(1)} %get-tuple-element.5, f32[128]{0:T(128)S(1)} %get-tuple-element.6), kind=kOutput, calls=%fused_computation.20 | convolution fusion | flops 1610645504 | bytes 16778240 | tf_op jit(solution)/shard_map/labc,ck->labk/dot_general | solution.py:23
  6.9 4.8 %fusion.3 = f32[128,2,64,128]{3,0,2,1:T(8,128)S(1)} fusion(f32[128,2,64,128]{3,0,2,1:T(8,128)S(1)} %fusion.21, f32[128]{0:T(128)S(1)} %get-tuple-element.5, f32[128]{0:T(128)S(1)} %get-tuple-element.6), kind=kOutput, calls=%fused_computation.4 | convolution fusion | flops 1610645504 | bytes 16778240 | tf_op jit(solution)/shard_map/labk,bj->jlak/dot_general | solution.py:23
  11.7 8.3 %copy.37 = f32[128,2,64,128]{3,2,1,0:T(8,128)} copy(f32[128,2,64,128]{3,0,2,1:T(8,128)S(1)} %fusion.3) | data formatting | bytes 16777216 | tf_op jit(solution)/shard_map/labk,bj->jlak/dot_general | solution.py:23
  20.0 7.5 %all-to-all-start = ((f32[128,2,64,128]{3,2,1,0:T(8,128)}), f32[128,2,64,128]{3,2,1,0:T(8,128)}, u32[]{:S(2)}, u32[]{:S(2)}) async-start(f32[128,2,64,128]{3,2,1,0:T(8,128)} %copy.37), calls=%async_computation | async-start | bytes 16777216 | tf_op jit(solution)/shard_map/all_to_all | solution.py:42
  27.5 0.1 dynamic_slice.4
  27.6 0.6 dynamic-slice
  28.9 0.2 dynamic-update-slice
  29.1 182.8 %all-reduce = s32[32]{0:T(128)S(1)} all-reduce(s32[32]{0:T(128)S(1)} %dynamic-update-slice), channel_id=1, replica_groups=mesh['tm'=16,'space'=2] {'tm'}, use_global_device_ids=true, to_apply=%add | all-reduce | flops 32 | bytes 256
  212.0 0.1 broadcast_add_fusion.1
  212.0 0.1 broadcast_add_fusion
  212.1 0.0 all-to-all-done
  212.1 4.2 copy.38
  216.4 8.5 %fusion.17 = f32[4,32,128,128]{3,1,2,0:T(8,128)S(1)} fusion(f32[4,32,128,128]{3,2,1,0:T(8,128)S(1)} %bitcast.57, f32[32,32]{1,0:T(8,128)S(1)} %copy-done), kind=kOutput, calls=%fused_computation.18 | convolution fusion | flops 402653184 | bytes 16781312 | tf_op jit(solution)/shard_map/lm,jmak->jlak/dot_general | solution.py:23
  224.9 8.8 %fusion.9 = f32[128,4,32,128]{3,0,2,1:T(8,128)S(1)} fusion(f32[4,32,128,128]{3,1,2,0:T(8,128)S(1)} %fusion.17, f32[128]{0:T(128)S(1)} %get-tuple-element.5, f32[128]{0:T(128)S(1)} %get-tuple-element.6), kind=kOutput, calls=%fused_computation.10 | convolution fusion | flops 1610645504 | bytes 16778240 | tf_op jit(solution)/shard_map/jlak,ai->jlik/dot_general | solution.py:23
  233.7 0.0 copy-start.2
  233.7 5.7 %fusion.16 = f32[4,32,128,128]{3,2,1,0:T(8,128)S(1)} fusion(f32[128,4,32,128]{3,0,2,1:T(8,128)S(1)} %fusion.9, f32[128]{0:T(128)S(1)} %multiply_subtract_fusion, f32[4,32,128]{2,1,0:T(8,128)S(1)} %broadcast_add_fusion, f32[128]{0:T(128)S(1)} %get-tuple-element.5, f32[128]{0:T(128)S(1)} %get-tuple-element.6), kind=kOutput, calls=%fused_computation.17 | convolution fusion | flops 1614839808 | bytes 16844288 | tf_op jit(solution)/shard_map/jlik,ia->jlak/dot_general | solution.py:23
  239.4 0.0 copy-done.2
  239.4 8.8 %fusion.7 = f32[4,128,128,32]{2,3,1,0:T(8,128)S(1)} fusion(f32[4,32,128,128]{3,2,1,0:T(8,128)S(1)} %fusion.16, f32[32,32]{1,0:T(8,128)S(1)} %copy-done.2), kind=kOutput, calls=%fused_computation.8 | convolution fusion | flops 402653184 | bytes 16781312 | tf_op jit(solution)/shard_map/lm,jmak->jlak/dot_general | solution.py:23
  248.2 4.9 %copy.44 = f32[4,16,2,2,64,128]{5,4,2,0,3,1:T(8,128)S(1)} copy(f32[4,16,2,2,64,128]{5,2,1,4,3,0:T(2,128)S(1)} %bitcast.58) | data formatting | bytes 16777216 | tf_op jit(solution)/shard_map/reshape | solution.py:60
  253.1 190.3 %all_to_all.10 = f32[128,2,64,128]{3,2,1,0:T(8,128)S(1)} all-to-all(f32[128,2,64,128]{3,2,1,0:T(8,128)S(1)} %bitcast.59), channel_id=1, replica_groups=mesh['tm'=16,'space'=2] {'tm','space'}, dimensions={0} | all-to-all | bytes 16777216 | tf_op jit(solution)/shard_map/all_to_all | solution.py:62
  443.4 8.6 %fusion.5 = f32[128,2,64,128]{3,0,2,1:T(8,128)S(1)} fusion(f32[128,2,64,128]{3,2,1,0:T(8,128)S(1)} %all_to_all.10, f32[128]{0:T(128)S(1)} %get-tuple-element.5, f32[128]{0:T(128)S(1)} %get-tuple-element.6), kind=kOutput, calls=%fused_computation.6 | convolution fusion | flops 1610645504 | bytes 16778240 | tf_op jit(solution)/shard_map/jlak,jb->labk/dot_general | solution.py:23
  452.0 6.2 %fusion = f32[2,64,128,128]{3,2,1,0:T(8,128)} fusion(f32[128,2,64,128]{3,0,2,1:T(8,128)S(1)} %fusion.5, f32[128]{0:T(128)S(1)} %get-tuple-element.5, f32[128]{0:T(128)S(1)} %get-tuple-element.6), kind=kOutput, calls=%fused_computation | convolution fusion | flops 1610645504 | bytes 16778240 | tf_op jit(solution)/shard_map/labk,kc->labc/dot_general | solution.py:23
  458.2 0.0 copy-done.1
  (10 shorter events, 0.1 us)
Async XLA Ops:
  0.0 216.4 %copy-start = (f32[32,32]{1,0:T(8,128)S(1)}, f32[32,32]{1,0:T(8,128)}, u32[]{:S(2)}) copy-start(f32[32,32]{1,0:T(8,128)} %param.7) | copy-start | bytes 12292
  20.0 7.6 %copy-start.4 = (u32[32]{0:T(128)S(1)}, u32[32]{0:T(128)}, u32[]{:S(2)}) copy-start(u32[32]{0:T(128)} %constant.56) | copy-start | bytes 388
  20.0 8.9 %copy-start.3 = (s32[2]{0:T(128)S(1)}, s32[2]{0:T(128)}, u32[]{:S(2)}) copy-start(s32[2]{0:T(128)} %param.5) | copy-start | bytes 28
  20.0 192.2 %all-to-all-start = ((f32[128,2,64,128]{3,2,1,0:T(8,128)}), f32[128,2,64,128]{3,2,1,0:T(8,128)}, u32[]{:S(2)}, u32[]{:S(2)}) async-start(f32[128,2,64,128]{3,2,1,0:T(8,128)} %copy.37), calls=%async_computation | async-start | bytes 16777216 | tf_op jit(solution)/shard_map/all_to_all | solution.py:42
  233.7 5.7 %copy-start.2 = (f32[32,32]{1,0:T(8,128)S(1)}, f32[32,32]{1,0:T(8,128)}, u32[]{:S(2)}) copy-start(f32[32,32]{1,0:T(8,128)} %param.6) | copy-start | bytes 12292
  443.4 14.9 %copy-start.1 = (f32[32,32]{1,0:T(8,128)S(1)}, f32[32,32]{1,0:T(8,128)}, u32[]{:S(2)}) copy-start(f32[32,32]{1,0:T(8,128)} %param.7) | copy-start | bytes 12292

commit v2 on v1

v2 whole, which is shorter than its diff:
```python
import jax
import jax.numpy as jnp
from jax import lax
from jax.sharding import PartitionSpec as P

split_mode = lax.Precision.HIGH


def sine_matrix(length):
    ordinal = jnp.arange(length, dtype=jnp.float32) + 1.0
    angle_step = jnp.pi / (length + 1)
    return jnp.sqrt(2.0 / (length + 1.0)) * jnp.sin(
        angle_step * ordinal[:, None] * ordinal[None, :]
    )


def eigen_values(length):
    ordinal = jnp.arange(length, dtype=jnp.float32) + 1.0
    return 2.0 - 2.0 * jnp.cos(jnp.pi * ordinal / (length + 1))


def product(formula, left, right):
    return jnp.einsum(formula, left, right, precision=split_mode)


def body(times, slabs, chunks, forcing, exponents, mixing, unmixing):
    own_steps, slab, length, _ = forcing.shape
    devices = times * slabs
    part = length // chunks
    rows = max(1, part // devices)
    pieces = max(1, devices // part)
    width = length // pieces
    everyone = ("tm", "space")
    sine = sine_matrix(length)
    eigen = eigen_values(length)
    all_exponents = lax.all_gather(exponents, "tm", axis=0, tiled=True)
    first_sine, all_exponents = lax.optimization_barrier((sine, all_exponents))
    shifts = 2.0 ** (all_exponents.astype(jnp.float32) / 4.0)
    device = lax.axis_index("tm") * slabs + lax.axis_index("space")
    own_columns = lax.dynamic_slice_in_dim(eigen, device % pieces * width, width)

    def spread(field, chunk):
        own_sine = first_sine[:, chunk * part : (chunk + 1) * part]
        field = product("labk,bj->jlak", field, own_sine)
        field = field.reshape(part, own_steps, slab, pieces, width).transpose(0, 3, 1, 2, 4)
        field = field.reshape(part * pieces, own_steps, slab, width)
        return lax.all_to_all(field, everyone, split_axis=0, concat_axis=0, tiled=True)

    def solve(field, chunk):
        field = field.reshape(times, slabs, rows, own_steps, slab, width)
        field = field.transpose(2, 0, 3, 1, 4, 5).reshape(rows, times * own_steps, length, width)
        field = product("lm,jmak->jlak", unmixing, field)
        field = product("jlak,ai->jlik", field, sine)
        first = chunk * part + device * rows // pieces
        own_rows = lax.dynamic_slice_in_dim(eigen, first, rows)
        denom = (
            shifts[None, :, None, None]
            + eigen[None, None, :, None]
            + own_rows[:, None, None, None]
            + own_columns[None, None, None, :]
        )
        field = product("jlik,ia->jlak", field / denom, sine)
        field = product("lm,jmak->jlak", mixing, field)
        field = field.reshape(rows, times, own_steps, slabs, slab, width)
        field = field.transpose(1, 3, 0, 2, 4, 5).reshape(part * pieces, own_steps, slab, width)
        return lax.all_to_all(field, everyone, split_axis=0, concat_axis=0, tiled=True)

    def gather(field, chunk):
        field = field.reshape(part, pieces, own_steps, slab, width).transpose(0, 2, 3, 1, 4)
        field = field.reshape(part, own_steps, slab, length)
        return product("jlak,jb->labk", field, sine[chunk * part : (chunk + 1) * part])

    field = product("labc,ck->labk", forcing, sine)
    sent = [spread(field, chunk) for chunk in range(chunks)]
    solved = [solve(held, chunk) for chunk, held in enumerate(sent)]
    field = sum(gather(held, chunk) for chunk, held in enumerate(solved))
    return product("labk,kc->labc", field, sine)


def solution(mesh):
    placed = (P("tm", "space", None, None), P("tm"), P(), P())

    def run(*arrays):
        return body(mesh.shape["tm"], mesh.shape["space"], 2, *arrays)

    return jax.shard_map(
        run, mesh=mesh, in_specs=placed, out_specs=P("tm", "space", None, None), check_vma=False
    )
```

time: 468 us -> 447 us (0.955)
  blocking collectives: 373 us -> 13.8 us
  waiting for transfers between devices: 0.01 us -> 292 us
  matrix products: 58.3 us -> 89.7 us
  starting transfers between devices: 7.46 us -> 17.9 us
  local copies, waits for them, and re-layouts: 18.3 us -> 24.9 us
    all_to_all x1 -> x4, waiting for transfers between devices: 0.01 us -> 292 us  [the longest x2 152 us: solve(): lax.all_to_all(field, everyone, split_axis=0, concat_axis=0, tiled=True)]
    all_to_all x1 -> x0, blocking collectives: 190 us -> none  [body(): lax.all_to_all(field, everyone, split_axis=0, concat_axis=0, tiled=True)]
    unnamed x1 -> x0, blocking collectives: 183 us -> none
    dot_general x8 -> x14, matrix products: 58.3 us -> 89.7 us  [product(): return jnp.einsum(formula, left, right, precision=split_mode)]
    optimization_barrier x0 -> x1, blocking collectives: none -> 13.8 us  [body(): first_sine, all_exponents = lax.optimization_barrier((sine, all_exponents))]
    all_to_all x1 -> x4, starting transfers between devices: 7.46 us -> 17.9 us  [the longest x2 9.47 us: solve(): lax.all_to_all(field, everyone, split_axis=0, concat_axis=0, tiled=True)]
  transfers between devices with their start and end apart: 1 -> 4, of which waited for: 0 -> 4; matrix products, arithmetic and copies ran while one was open for 0% -> 19% of each run, Pallas kernels for 0% -> 0%
where the time goes in v2:
time: 447 us; the launch traced here: 440 us
  waiting for transfers between devices  292 us (65%)
  matrix products  89.7 us (20%)
  local copies, waits for them, and re-layouts  24.9 us (6%)
  starting transfers between devices  17.9 us (4%)
  blocking collectives  13.8 us (3%)
    all_to_all x2, waiting for transfers between devices, solve(): lax.all_to_all(field, everyone, split_axis=0, concat_axis=0, tiled=True)  152 us
    all_to_all x2, waiting for transfers between devices, spread(): lax.all_to_all(field, everyone, split_axis=0, concat_axis=0, tiled=True)  140 us
    dot_general x14, matrix products, product(): return jnp.einsum(formula, left, right, precision=split_mode)  89.7 us
    optimization_barrier x1, blocking collectives, body(): first_sine, all_exponents = lax.optimization_barrier((sine, all_exponents))  13.8 us
    all_to_all x2, starting transfers between devices, solve(): lax.all_to_all(field, everyone, split_axis=0, concat_axis=0, tiled=True)  9.47 us
  transfers between devices with their start and end apart: 4, of which 4 were waited for; matrix products, arithmetic and copies ran while one was open for 19% of the time, Pallas kernels for 0%

profile of v2, /device:TPU:0, one launch (start us, length us, event | category | flops | bytes accessed | tf_op | source)
XLA Modules:
  0.0 440.1 jit_solution(4386645794117447329)
XLA Ops:
  2.8 13.8 %all-reduce = s32[32]{0:T(128)S(1)} all-reduce(s32[32]{0:T(128)S(1)} %dynamic-update-slice), channel_id=1, replica_groups=mesh['tm'=16,'space'=2] {'tm'}, use_global_device_ids=true, to_apply=%add | all-reduce | flops 32 | bytes 256 | tf_op jit(solution)/shard_map/optimization_barrier | solution.py:37
  16.8 6.8 %fusion.44 = f32[128,2,64,128]{3,0,2,1:T(8,128)S(1)} fusion(f32[2,64,128,128]{3,2,1,0:T(8,128)} %param.4, f32[128]{0:T(128)S(1)} %get-tuple-element.13, f32[128]{0:T(128)S(1)} %get-tuple-element.14), kind=kOutput, calls=%fused_computation.44 | convolution fusion | flops 1610645504 | bytes 16778240 | tf_op jit(solution)/shard_map/labc,ck->labk/dot_general | solution.py:23
  23.6 4.8 %fusion.4 = f32[64,2,64,128]{3,0,2,1:T(8,128)S(1)} fusion(f32[128,2,64,128]{3,0,2,1:T(8,128)S(1)} %fusion.44, f32[128,128]{0,1:T(8,128)S(1)} %sine_multiply_fusion), kind=kOutput, calls=%fused_computation.4 | convolution fusion | flops 805306368 | bytes 12615680 | tf_op jit(solution)/shard_map/labk,bj->jlak/dot_general | solution.py:23
  28.4 4.4 %copy.52 = f32[64,2,64,128]{3,2,1,0:T(8,128)} copy(f32[64,2,64,128]{3,0,2,1:T(8,128)S(1)} %fusion.4) | data formatting | bytes 8388608 | tf_op jit(solution)/shard_map/labk,bj->jlak/dot_general | solution.py:23
  36.7 6.8 %fusion.2 = f32[64,2,64,128]{3,0,2,1:T(8,128)S(1)} fusion(f32[128,2,64,128]{3,0,2,1:T(8,128)} %copy-done.2, f32[128,128]{0,1:T(8,128)S(1)} %sine_multiply_fusion), kind=kOutput, calls=%fused_computation.2 | convolution fusion | flops 805306368 | bytes 12615680 | tf_op jit(solution)/shard_map/labk,bj->jlak/dot_general | solution.py:23
  43.5 4.4 copy.61
  47.9 82.5 %all-to-all-done = f32[64,2,64,128]{3,2,1,0:T(8,128)} async-done(((f32[64,2,64,128]{3,2,1,0:T(8,128)}), f32[64,2,64,128]{3,2,1,0:T(8,128)}, u32[]{:S(2)}, u32[]{:S(2)}) %all-to-all-start) | async-done | bytes 4194336 | tf_op jit(solution)/shard_map/all_to_all | solution.py:47
  130.4 4.6 %all-to-all-start.2 = ((f32[64,2,64,128]{3,2,1,0:T(8,128)}), f32[64,2,64,128]{3,2,1,0:T(8,128)}, u32[]{:S(2)}, u32[]{:S(2)}) async-start(f32[64,2,64,128]{3,2,1,0:T(8,128)} %copy.61), calls=%async_computation.2 | async-start | bytes 8388608 | tf_op jit(solution)/shard_map/all_to_all | solution.py:47
  137.8 4.2 fusion.27
  142.0 4.5 %fusion.21 = f32[128,2,32,128]{3,0,2,1:T(8,128)S(1)} fusion(f32[2,32,128,128]{3,1,2,0:T(8,128)S(1)} %fusion.27, f32[128]{0:T(128)S(1)} %get-tuple-element.13, f32[128]{0:T(128)S(1)} %get-tuple-element.14), kind=kOutput, calls=%fused_computation.23 | convolution fusion | flops 805339136 | bytes 8389632 | tf_op jit(solution)/shard_map/jlak,ai->jlik/dot_general | solution.py:23
  149.4 16.9 %fusion.19 = f32[2,128,128,32]{2,3,1,0:T(8,128)S(1)} fusion(f32[2,32,128,128]{3,2,1,0:T(8,128)S(1)} %fusion.33, f32[32,32]{1,0:T(8,128)S(1)} %copy-done.4), kind=kOutput, calls=%fused_computation.21 | convolution fusion | flops 201326592 | bytes 8392704 | tf_op jit(solution)/shard_map/lm,jmak->jlak/dot_general | solution.py:23
  166.3 4.4 %copy.57 = f32[2,16,2,2,64,128]{5,4,2,0,3,1:T(8,128)} copy(f32[2,16,2,2,64,128]{5,2,1,4,3,0:T(2,128)S(1)} %bitcast.97) | data formatting | bytes 8388608 | tf_op jit(solution)/shard_map/reshape | solution.py:64
  170.7 57.9 %all-to-all-done.2 = f32[64,2,64,128]{3,2,1,0:T(8,128)} async-done(((f32[64,2,64,128]{3,2,1,0:T(8,128)}), f32[64,2,64,128]{3,2,1,0:T(8,128)}, u32[]{:S(2)}, u32[]{:S(2)}) %all-to-all-start.2) | async-done | bytes 4194336 | tf_op jit(solution)/shard_map/all_to_all | solution.py:47
  228.6 4.7 %all-to-all-start.1 = ((f32[64,2,64,128]{3,2,1,0:T(8,128)}), f32[64,2,64,128]{3,2,1,0:T(8,128)}, u32[]{:S(2)}, u32[]{:S(2)}) async-start(f32[64,2,64,128]{3,2,1,0:T(8,128)} %bitcast.94), calls=%async_computation.1 | async-start | bytes 8388608 | tf_op jit(solution)/shard_map/all_to_all | solution.py:66
  235.9 4.2 fusion.30
  240.1 4.5 %fusion.13 = f32[128,2,32,128]{3,0,2,1:T(8,128)S(1)} fusion(f32[2,32,128,128]{3,1,2,0:T(8,128)S(1)} %fusion.30, f32[128]{0:T(128)S(1)} %get-tuple-element.13, f32[128]{0:T(128)S(1)} %get-tuple-element.14), kind=kOutput, calls=%fused_computation.15 | convolution fusion | flops 805339136 | bytes 8389632 | tf_op jit(solution)/shard_map/jlak,ai->jlik/dot_general | solution.py:23
  247.4 4.4 %fusion.11 = f32[2,128,128,32]{2,3,1,0:T(8,128)S(1)} fusion(f32[2,32,128,128]{3,2,1,0:T(8,128)S(1)} %fusion.34, f32[32,32]{1,0:T(8,128)S(1)} %copy-done.4), kind=kOutput, calls=%fused_computation.13 | convolution fusion | flops 201326592 | bytes 8392704 | tf_op jit(solution)/shard_map/lm,jmak->jlak/dot_general | solution.py:23
  251.8 4.4 copy.66
  256.2 70.8 %all-to-all-done.1 = f32[64,2,64,128]{3,2,1,0:T(8,128)} async-done(((f32[64,2,64,128]{3,2,1,0:T(8,128)}), f32[64,2,64,128]{3,2,1,0:T(8,128)}, u32[]{:S(2)}, u32[]{:S(2)}) %all-to-all-start.1) | async-done | bytes 4194336 | tf_op jit(solution)/shard_map/all_to_all | solution.py:66
  327.0 4.7 %all-to-all-start.3 = ((f32[64,2,64,128]{3,2,1,0:T(8,128)}), f32[64,2,64,128]{3,2,1,0:T(8,128)}, u32[]{:S(2)}, u32[]{:S(2)}) async-start(f32[64,2,64,128]{3,2,1,0:T(8,128)} %bitcast.95), calls=%async_computation.3 | async-start | bytes 8388608 | tf_op jit(solution)/shard_map/all_to_all | solution.py:66
  331.8 12.7 %fusion.17 = f32[128,2,64,128]{3,0,2,1:T(8,128)} fusion(f32[64,2,64,128]{3,2,1,0:T(8,128)} %all-to-all-done.1, f32[128,128]{0,1:T(8,128)S(1)} %sine_multiply_fusion), kind=kOutput, calls=%fused_computation.19 | convolution fusion | flops 805306368 | bytes 12648448 | tf_op jit(solution)/shard_map/jlak,jb->labk/dot_general | solution.py:23
  344.4 81.0 %all-to-all-done.3 = f32[64,2,64,128]{3,2,1,0:T(8,128)} async-done(((f32[64,2,64,128]{3,2,1,0:T(8,128)}), f32[64,2,64,128]{3,2,1,0:T(8,128)}, u32[]{:S(2)}, u32[]{:S(2)}) %all-to-all-start.3) | async-done | bytes 4194336 | tf_op jit(solution)/shard_map/all_to_all | solution.py:66
  425.4 8.1 %fusion.9 = f32[128,2,64,128]{3,0,2,1:T(8,128)S(1)} fusion(f32[64,2,64,128]{3,2,1,0:T(8,128)} %all-to-all-done.3, f32[128,128]{0,1:T(8,128)S(1)} %sine_multiply_fusion), kind=kOutput, calls=%fused_computation.11 | convolution fusion | flops 805306368 | bytes 12648448 | tf_op jit(solution)/shard_map/jlak,jb->labk/dot_general | solution.py:23
  433.5 6.2 %fusion = f32[2,64,128,128]{3,2,1,0:T(8,128)} fusion(f32[128,2,64,128]{3,0,2,1:T(8,128)S(1)} %copy-done.3, f32[128,2,64,128]{3,0,2,1:T(8,128)S(1)} %fusion.9, f32[128]{0:T(128)S(1)} %get-tuple-element.13, f32[128]{0:T(128)S(1)} %get-tuple-element.14), kind=kOutput, calls=%fused_computation | convolution fusion | flops 1612742656 | bytes 25166848 | tf_op jit(solution)/shard_map/labk,kc->labc/dot_general | solution.py:23
  (25 shorter events, 17.2 us)
Async XLA Ops:
  0.0 137.8 %copy-start = (f32[32,32]{1,0:T(8,128)S(1)}, f32[32,32]{1,0:T(8,128)}, u32[]{:S(2)}) copy-start(f32[32,32]{1,0:T(8,128)} %param.7) | copy-start | bytes 12292
  23.6 4.8 %copy-start.2 = (f32[128,2,64,128]{3,0,2,1:T(8,128)}, f32[128,2,64,128]{3,0,2,1:T(8,128)S(1)}, u32[]{:S(2)}) copy-start(f32[128,2,64,128]{3,0,2,1:T(8,128)S(1)} %fusion.44) | copy-start | bytes 25165828
  32.8 97.5 %all-to-all-start = ((f32[64,2,64,128]{3,2,1,0:T(8,128)}), f32[64,2,64,128]{3,2,1,0:T(8,128)}, u32[]{:S(2)}, u32[]{:S(2)}) async-start(f32[64,2,64,128]{3,2,1,0:T(8,128)} %copy.52), calls=%async_computation | async-start | bytes 8388608 | tf_op jit(solution)/shard_map/all_to_all | solution.py:47
  130.4 98.3 %all-to-all-start.2 = ((f32[64,2,64,128]{3,2,1,0:T(8,128)}), f32[64,2,64,128]{3,2,1,0:T(8,128)}, u32[]{:S(2)}, u32[]{:S(2)}) async-start(f32[64,2,64,128]{3,2,1,0:T(8,128)} %copy.61), calls=%async_computation.2 | async-start | bytes 8388608 | tf_op jit(solution)/shard_map/all_to_all | solution.py:47
  146.5 2.9 copy-start.4
  228.6 98.4 %all-to-all-start.1 = ((f32[64,2,64,128]{3,2,1,0:T(8,128)}), f32[64,2,64,128]{3,2,1,0:T(8,128)}, u32[]{:S(2)}, u32[]{:S(2)}) async-start(f32[64,2,64,128]{3,2,1,0:T(8,128)} %bitcast.94), calls=%async_computation.1 | async-start | bytes 8388608 | tf_op jit(solution)/shard_map/all_to_all | solution.py:66
  327.0 98.4 %all-to-all-start.3 = ((f32[64,2,64,128]{3,2,1,0:T(8,128)}), f32[64,2,64,128]{3,2,1,0:T(8,128)}, u32[]{:S(2)}, u32[]{:S(2)}) async-start(f32[64,2,64,128]{3,2,1,0:T(8,128)} %bitcast.95), calls=%async_computation.3 | async-start | bytes 8388608 | tf_op jit(solution)/shard_map/all_to_all | solution.py:66
  425.4 8.1 %copy-start.3 = (f32[128,2,64,128]{3,0,2,1:T(8,128)S(1)}, f32[128,2,64,128]{3,0,2,1:T(8,128)}, u32[]{:S(2)}) copy-start(f32[128,2,64,128]{3,0,2,1:T(8,128)} %fusion.17) | copy-start | bytes 25165828
  433.5 6.2 %copy-start.1 = (f32[32,32]{1,0:T(8,128)S(1)}, f32[32,32]{1,0:T(8,128)}, u32[]{:S(2)}) copy-start(f32[32,32]{1,0:T(8,128)} %param.7) | copy-start | bytes 12292
